TPU v7x, 32 devices: a whole 2x2x4 slice. The times are simulated.
32 devices in a mesh: seq: 16 (over z, y, x), slide: 2 (over core).
Axes of the slice: x: 2, y: 2, z: 4, core: 2. Of those that a mesh axis runs over, the one named last changes fastest.
Arguments:
- tile_embed: bfloat16 [16384, 768], P(('slide', 'seq')), parts along dimension 0, may hold values from -6 to 6
- valid_tiles: int32 [2], P('slide'), parts along dimension 0, may hold values from 4096 to 8192
- offsets: int32 [16], replicated, may hold values from 0 to 15
- norm_gain: float32 [768], replicated, may hold values from 0.1 to 1.9
- w_qkv: bfloat16 [768, 2304], replicated
- sub_gain: float32 [768], replicated, may hold values from 0.1 to 1.9
- w_out: bfloat16 [768, 768], replicated, may hold values from -0.21875 to 0.21875
Outputs:
- encoded: bfloat16 [16384, 768], P(('slide', 'seq')), parts along dimension 0
There are 2 independent parts, one for each index of `slide`. A program takes and returns all parts, laid end to end along the dimension named above; an argument that names none is the same for every part. Nothing has to cross between parts.
All inputs are finite; a program needn't handle non-finite values.
Results may differ from a plain program's by a relative error of at most 0.0078.
Values may be sent and summed in bfloat16 or wider, within the bound.
A program may use at most 128 MiB of HBM per device.

v0:
```python
import functools

import jax
import jax.numpy as jnp
import numpy as np
from jax import lax
from jax.experimental import pallas as pl
from jax.experimental.pallas import tpu as pltpu
from jax.sharding import PartitionSpec as P

MIDDLE_DILATION = 4
FAR_DILATION = 16
NEGATIVE = -1e30
EPSILON = 1e-05
LOG2E = 1.4426950408889634
AUG = 16
VMEM_LIMIT = 60 * 1024 * 1024


def layer_norm_rows(x, gain):
    average = jnp.mean(x, axis=-1, keepdims=True)
    centred = x - average
    variance = jnp.mean(centred * centred, axis=-1, keepdims=True)
    return centred * lax.rsqrt(variance + EPSILON) * gain


def project_into(dst, x_ref, gain_ref, w_ref, chunk, skip=0):
    normed = layer_norm_rows(x_ref[...].astype(jnp.float32), gain_ref[...]).astype(jnp.bfloat16)

    @pl.loop(0, (w_ref.shape[0] - skip) // chunk)
    def _(i):
        rows = pl.ds(pl.multiple_of(i * chunk, chunk), chunk)
        dst[rows, :] = lax.dot_general(
            w_ref[pl.ds(pl.multiple_of(i * chunk + skip, chunk), chunk), :], normed, (((1,), (1,)), ((), ())), preferred_element_type=jnp.float32
        ).astype(jnp.bfloat16)


def project_kernel(heads, offs, x_ref, gain_ref, w_ref, proj_ref, mid_ref, fark_ref, farv_ref, far_scr):
    rows, width = x_ref.shape
    size = width // heads
    lanes = rows // MIDDLE_DILATION
    few = rows // FAR_DILATION
    project_into(proj_ref, x_ref, gain_ref, w_ref, 256)
    src = lax.broadcasted_iota(jnp.int32, (lanes, lanes), 0)
    dst = lax.broadcasted_iota(jnp.int32, (lanes, lanes), 1)
    for head in range(heads):
        phase = offs[head] % FAR_DILATION
        quarter = phase % MIDDLE_DILATION
        shift = (phase // MIDDLE_DILATION) * few
        pick = ((src == dst + shift) & (dst < few)).astype(jnp.bfloat16)
        for part in range(2):
            base = part * width + head * size
            block = proj_ref[
                width + base : width + base + size,
                pl.ds(pl.multiple_of(quarter * lanes, lanes), lanes),
            ]
            mid_ref[base : base + size, :] = block
            far_scr[base : base + size, :] = jnp.dot(
                block, pick, preferred_element_type=jnp.float32
            )
    fark_ref[...] = far_scr[:width, :].T[:few].astype(jnp.bfloat16)
    farv_ref[...] = far_scr[width:, :].T[:few].astype(jnp.bfloat16)


def aug_rows(first, lanes, second=None):
    spot = lax.broadcasted_iota(jnp.int32, (AUG, lanes), 0)
    rows = jnp.where(spot == 0, first, 0.0)
    if second is not None:
        rows = jnp.where(spot == 1, second, rows)
    return rows.astype(jnp.bfloat16)


def weighted_values(value, weight):
    scaled = (value.astype(jnp.float32) * weight).astype(jnp.bfloat16)
    return jnp.concatenate([scaled, aug_rows(weight, value.shape[1])], axis=0)


def scores_of(keys, queries):
    return lax.dot_general(
        keys, queries, (((0,), (0,)), ((), ())), preferred_element_type=jnp.float32
    )


def own_kernel(scale, per_step, size, valid, q_ref, k_ref, v_ref, pos_ref, out_ref):
    lanes = q_ref.shape[1]
    alive = pos_ref[...] + lax.axis_index("seq") * lanes < valid[0]
    bias = aug_rows(jnp.where(alive, 0.0, NEGATIVE), lanes)
    weight = jnp.where(alive, 1.0, 0.0)
    unit = aug_rows(jnp.ones((1, lanes), jnp.float32), lanes)
    for i in range(per_step):
        part = slice(i * size, (i + 1) * size)
        scores = scores_of(
            jnp.concatenate([k_ref[part, :], bias], axis=0),
            jnp.concatenate([q_ref[part, :], unit], axis=0),
        )
        top = jnp.max(scores, axis=0, keepdims=True)
        p = jnp.exp2((scores - top) * scale).astype(jnp.bfloat16)
        base = i * (size + AUG)
        out_ref[base : base + size + AUG, :] = jnp.dot(
            weighted_values(v_ref[part, :], weight), p, preferred_element_type=jnp.float32
        )
        out_ref[base + size + 1 : base + size + 2, :] = top


def rest_kernel(
    heads, scale, per_step, far_span, middle, offs, valid,
    x_ref, xp_ref, gain_ref, w_ref, q_ref, k_ref, v_ref, own_ref, ppos_ref,
    *rest,
):
    others = middle - 2
    midk, midv = rest[:others], rest[others : 2 * others]
    fark_ref, farv_ref, extra_ref, subgain_ref, wout_ref = rest[2 * others : 2 * others + 5]
    out_ref, kvp, far_t, o_scr, att = rest[2 * others + 5 :]
    rows, width = x_ref.shape
    size = width // heads
    lanes = rows // MIDDLE_DILATION
    few = rows // FAR_DILATION
    step = pl.program_id(0)

    @pl.when(step == 0)
    def _():
        project_into(kvp, xp_ref, gain_ref, w_ref, 256, width)
        for i in range(fark_ref.shape[0] // 128):
            far_t[:width, i * 128 : (i + 1) * 128] = fark_ref[i * 128 : (i + 1) * 128, :].T
            far_t[width:, i * 128 : (i + 1) * 128] = farv_ref[i * 128 : (i + 1) * 128, :].T

    me = lax.axis_index("seq")
    alive = ppos_ref[...] + (me ^ 1) * rows < valid[0]
    bias = aug_rows(jnp.where(alive, 0.0, NEGATIVE), rows)
    weight = jnp.where(alive, 1.0, 0.0)
    unit = aug_rows(jnp.ones((1, rows), jnp.float32), rows)
    is_far = extra_ref[1:2, :]
    device = extra_ref[2:3, :] ^ me
    start = extra_ref[0:1, :] + device * rows
    times = jnp.where((is_far == 1) & (device // far_span == me // far_span), 2, 1)
    lane = lax.broadcasted_iota(jnp.int32, (1, lanes), 1)
    for i in range(per_step):
        head = step * per_step + i
        part = slice(i * size, (i + 1) * size)
        base = i * (size + AUG)
        both = slice(base, base + size + AUG)
        phase = offs[head] % FAR_DILATION
        quarter = phase % MIDDLE_DILATION
        cols = pl.ds(pl.multiple_of(quarter * lanes, lanes), lanes)
        krows = pl.ds(pl.multiple_of(head * size, AUG), size)
        vrows = pl.ds(pl.multiple_of(width + head * size, AUG), size)

        scores = scores_of(
            jnp.concatenate([kvp[krows, :], bias], axis=0),
            jnp.concatenate([q_ref[part, :], unit], axis=0),
        )
        own = own_ref[both, :]
        own_top = own[size + 1 : size + 2, :]
        top = jnp.maximum(own_top, jnp.max(scores, axis=0, keepdims=True))
        p = jnp.exp2((scores - top) * scale).astype(jnp.bfloat16)
        o_scr[both, :] = own * jnp.exp2((own_top - top) * scale) + jnp.dot(
            weighted_values(kvp[vrows, :], weight), p, preferred_element_type=jnp.float32
        )
        o_scr[base + size + 1 : base + size + 2, :] = top

        keys = jnp.concatenate(
            [k_ref[part, cols], kvp[krows, cols]]
            + [midk[g][part, :] for g in range(others)]
            + [far_t[krows, :]],
            axis=1,
        )
        values = jnp.concatenate(
            [v_ref[part, cols], kvp[vrows, cols]]
            + [midv[g][part, :] for g in range(others)]
            + [far_t[vrows, :]],
            axis=1,
        )
        spot = start + jnp.where(is_far == 1, phase, quarter)
        live = spot < valid[0]
        count = jnp.where(live, times, 0).astype(jnp.float32)
        keys = jnp.concatenate(
            [
                keys,
                aug_rows(
                    jnp.where(live, 0.0, NEGATIVE), keys.shape[1], is_far.astype(jnp.float32)
                ),
            ],
            axis=0,
        )
        mine = lane // few == phase // MIDDLE_DILATION
        queries = jnp.concatenate(
            [
                q_ref[part, cols],
                aug_rows(
                    jnp.ones((1, lanes), jnp.float32), lanes, jnp.where(mine, 0.0, NEGATIVE)
                ),
            ],
            axis=0,
        )
        more = scores_of(keys, queries)
        had = o_scr[both, cols]
        had_top = had[size + 1 : size + 2, :]
        new_top = jnp.maximum(had_top, jnp.max(more, axis=0, keepdims=True))
        p = jnp.exp2((more - new_top) * scale).astype(jnp.bfloat16)
        total = had * jnp.exp2((had_top - new_top) * scale) + jnp.dot(
            weighted_values(values, count), p, preferred_element_type=jnp.float32
        )
        o_scr[both, cols] = jnp.where(new_top > 0.5 * NEGATIVE, total, 0.0)
        done = o_scr[both, :]
        result = done[:size] / jnp.maximum(done[size : size + 1], 1.0)
        att[pl.ds(pl.multiple_of(head * size, AUG), size), :] = result.astype(jnp.bfloat16)

    @pl.when(step == pl.num_programs(0) - 1)
    def _():
        attended = att[...].astype(jnp.float32)
        average = jnp.mean(attended, axis=0, keepdims=True)
        centred = attended - average
        variance = jnp.mean(centred * centred, axis=0, keepdims=True)
        normed = centred * lax.rsqrt(variance + EPSILON) * subgain_ref[...]
        projected = jnp.dot(
            normed.T.astype(jnp.bfloat16), wout_ref[...], preferred_element_type=jnp.float32
        )
        out_ref[...] = (x_ref[...].astype(jnp.float32) + projected).astype(jnp.bfloat16)


def doubled(rows, bit, devices):
    pairs = [(d, d ^ (1 << bit)) for d in range(devices)]
    return jnp.concatenate([rows, lax.ppermute(rows, "seq", pairs)], axis=0)


def body(tile_embed, valid_tiles, offsets, norm_gain, w_qkv, sub_gain, w_out):
    devices = lax.axis_size("seq")
    me = lax.axis_index("seq")
    rows, width = tile_embed.shape
    heads = offsets.shape[0]
    size = width // heads
    lanes = rows // MIDDLE_DILATION
    few = rows // FAR_DILATION
    each = rows // devices
    middle = max(4, devices // 16)
    far_span = max(8, devices // 4)
    per_step = 2
    steps = heads // per_step
    scale = float(size) ** -0.5 * LOG2E

    w_t = w_qkv.T
    pieces = tile_embed.reshape(devices, each, width)
    arrived = lax.all_to_all(pieces, "seq", split_axis=0, concat_axis=0, tiled=True)
    groups = devices // FAR_DILATION
    x = arrived.reshape(groups, 4, 4, each, width).transpose(2, 1, 0, 3, 4).reshape(rows, width)
    xp = lax.ppermute(x, "seq", [(d, d ^ 1) for d in range(devices)])

    whole = lambda *shape: pl.BlockSpec(shape, lambda *_: (0,) * len(shape))
    smem = pl.BlockSpec(memory_space=pltpu.SMEM)
    gain = norm_gain.reshape(1, width)

    proj, mid, far_key, far_value = pl.pallas_call(
        functools.partial(project_kernel, heads),
        out_shape=(
            jax.ShapeDtypeStruct((3 * width, rows), jnp.bfloat16),
            jax.ShapeDtypeStruct((2 * width, lanes), jnp.bfloat16),
            jax.ShapeDtypeStruct((few, width), jnp.bfloat16),
            jax.ShapeDtypeStruct((few, width), jnp.bfloat16),
        ),
        in_specs=[smem] + [pl.BlockSpec(memory_space=pltpu.VMEM)] * 3,
        out_specs=(pl.BlockSpec(memory_space=pltpu.VMEM),) * 4,
        scratch_shapes=[pltpu.VMEM((2 * width, lanes), jnp.float32)],
        compiler_params=pltpu.CompilerParams(vmem_limit_bytes=VMEM_LIMIT),
        cost_estimate=pl.CostEstimate(
            flops=6 * rows * width * width, bytes_accessed=12 * width * width, transcendentals=0
        ),
        name="project",
    )(offsets, x, gain, w_t)

    mids = [
        lax.ppermute(mid, "seq", [(d, d ^ g) for d in range(devices)]) for g in range(2, middle)
    ]
    bits = devices.bit_length() - 1
    for bit in range(bits):
        far_key = doubled(far_key, bit, devices)
        far_value = doubled(far_value, bits - 1 - bit, devices)
    far_value = (
        far_value.reshape((2,) * bits + (few, width))
        .transpose(tuple(reversed(range(bits))) + (bits, bits + 1))
        .reshape(devices * few, width)
    )

    local = np.arange(rows, dtype=np.int32).reshape(each, groups, 4, 4).transpose(3, 2, 1, 0)
    local = local.reshape(1, rows)
    seats = np.arange(devices, dtype=np.int32)
    mid_rows = [np.tile(local[0, :lanes], middle), np.zeros(middle * lanes, np.int32),
                np.repeat(np.arange(middle, dtype=np.int32), lanes)]
    far_rows = [np.tile(local[0, :few], devices), np.ones(devices * few, np.int32),
                np.repeat(seats, few)]
    extra = np.concatenate([np.stack(mid_rows), np.stack(far_rows)], axis=1)
    extra_count = extra.shape[1]

    strip = per_step * size
    out_strip = per_step * (size + AUG)
    block = lambda part: pl.BlockSpec((strip, rows), lambda h: (part * steps + h, 0))
    own = pl.pallas_call(
        functools.partial(own_kernel, scale, per_step, size),
        grid=(steps,),
        out_shape=jax.ShapeDtypeStruct((heads * (size + AUG), rows), jnp.float32),
        in_specs=[smem, block(0), block(1), block(2), whole(1, rows)],
        out_specs=pl.BlockSpec((out_strip, rows), lambda h: (h, 0)),
        compiler_params=pltpu.CompilerParams(vmem_limit_bytes=VMEM_LIMIT),
        cost_estimate=pl.CostEstimate(
            flops=16 * rows * rows * width, bytes_accessed=8 * rows * width,
            transcendentals=heads * rows * rows,
        ),
        name="own_keys",
    )(valid_tiles, proj, proj, proj, jnp.asarray(local))

    out = pl.pallas_call(
        functools.partial(rest_kernel, heads, scale, per_step, far_span, middle),
        grid=(steps,),
        out_shape=jax.ShapeDtypeStruct((rows, width), jnp.bfloat16),
        in_specs=[
            smem, smem,
            whole(rows, width), whole(rows, width), whole(1, width), whole(3 * width, width),
            block(0), block(1), block(2),
            pl.BlockSpec((out_strip, rows), lambda h: (h, 0)),
            whole(1, rows),
            *[pl.BlockSpec((strip, lanes), lambda h: (h, 0))] * len(mids),
            *[pl.BlockSpec((strip, lanes), lambda h: (steps + h, 0))] * len(mids),
            whole(devices * few, width), whole(devices * few, width), whole(3, extra_count),
            whole(width, 1), whole(width, width),
        ],
        out_specs=whole(rows, width),
        scratch_shapes=[
            pltpu.VMEM((2 * width, rows), jnp.bfloat16),
            pltpu.VMEM((2 * width, devices * few), jnp.bfloat16),
            pltpu.VMEM((out_strip, rows), jnp.float32),
            pltpu.VMEM((width, rows), jnp.bfloat16),
        ],
        compiler_params=pltpu.CompilerParams(vmem_limit_bytes=VMEM_LIMIT),
        cost_estimate=pl.CostEstimate(
            flops=24 * rows * rows * width, bytes_accessed=20 * rows * width,
            transcendentals=heads * rows * rows,
        ),
        name="rest",
    )(
        offsets, valid_tiles, x, xp, gain, w_t, proj, proj, proj, own, jnp.asarray(local),
        *mids, *mids, far_key, far_value, jnp.asarray(extra), sub_gain.reshape(width, 1), w_out,
    )
    return (
        out.reshape(4, 4, groups, each, width).transpose(3, 2, 1, 0, 4).reshape(rows, width)
    )


def solution(mesh):
    return jax.shard_map(
        body,
        mesh=mesh,
        in_specs=(P(("slide", "seq"), None), P("slide"), P(), P(), P(), P(), P()),
        out_specs=P(("slide", "seq"), None),
        check_vma=False,
    )
```

profile of v0, /device:TPU:0, one launch (start us, length us, event | category | flops | bytes accessed | tf_op | source)
XLA Modules:
  0.0 114.0 jit_solution(4675630125280895580)
XLA Ops:
  0.0 8.3 %all-to-all-start = ((bf16[16,32,768]{2,1,0:T(8,128)(2,1)}), bf16[16,32,768]{2,1,0:T(8,128)(2,1)S(1)}, u32[]{:S(2)}, u32[]{:S(2)}) async-start(bf16[16,32,768]{2,1,0:T(8,128)(2,1)} %bitcast.24), calls=%async_computation | async-start | bytes 1572864 | tf_op jit(solution)/shard_map/all_to_all | solution.py:243
  9.0 1.3 %reshape.30.gain_ref = f32[1,768]{1,0:T(1,128)} reshape(f32[768]{0:T(1024)} %param.12) | data formatting | bytes 6144 | tf_op jit(solution)/shard_map/reshape | solution.py:250
  10.3 1.6 %reshape.36.rest_7_ = f32[768,1]{1,0:T(8,128)} reshape(f32[768]{0:T(1024)} %param.14) | data formatting | bytes 6144 | tf_op jit(solution)/shard_map/reshape | solution.py:340
  11.9 5.8 %copy.14 = bf16[768,2304]{0,1:T(8,128)(2,1)} copy(bf16[768,2304]{1,0:T(8,128)(2,1)} %param.13) | data formatting | bytes 7077888 | tf_op args[4]
  17.6 10.4 %all-to-all-done = bf16[16,32,768]{2,1,0:T(8,128)(2,1)S(1)} async-done(((bf16[16,32,768]{2,1,0:T(8,128)(2,1)}), bf16[16,32,768]{2,1,0:T(8,128)(2,1)S(1)}, u32[]{:S(2)}, u32[]{:S(2)}) %all-to-all-start) | async-done | bytes 786464 | tf_op jit(solution)/shard_map/all_to_all | solution.py:243
  28.0 0.1 copy.13
  28.1 0.0 copy-start
  28.1 0.6 collective-permute-start
  28.7 0.2 copy-done
  29.0 8.2 %project.1 = (bf16[2304,512]{1,0:T(8,128)(2,1)}, bf16[1536,128]{1,0:T(8,128)(2,1)}, bf16[32,768]{1,0:T(8,128)(2,1)}, bf16[32,768]{1,0:T(8,128)(2,1)}) custom-call(s32[16]{0:T(128)} %offs.3, bf16[512,768]{1,0:T(8,128)(2,1)} %bitcast.18, f32[1,768]{1,0:T(1,128)} %reshape.30.gain_ref, bf16[2304,768]{1,0:T(8,128)(2,1)} %bitcast.15), custom_call_target="tpu_custom_call" | custom-call | flops 1811939328 | bytes 7077888 | tf_op jit(solution)/shard_map/project/pallas_call | solution.py:252
  37.2 2.3 %collective-permute-start.2 = (bf16[1536,128]{1,0:T(8,128)(2,1)}, bf16[1536,128]{1,0:T(8,128)(2,1)S(1)}, u32[]{:S(2)}, u32[]{:S(2)}) collective-permute-start(bf16[1536,128]{1,0:T(8,128)(2,1)} %get-tuple-element.10), channel_id=1, source_target_pairs={{0,6},{2,4},{4,2},{6,0},{8,14},{10,12},{12,10},{14,8},{16,22},{18,... | collective-permute-start | bytes 1179656 | tf_op jit(solution)/shard_map/ppermute | solution.py:271
  39.5 0.4 collective-permute-start.1
  39.9 0.8 collective-permute-start.3
  40.7 2.4 %collective-permute-start.7 = (bf16[32,768]{1,0:T(8,128)(2,1)}, bf16[32,768]{1,0:T(8,128)(2,1)S(1)}, u32[]{:S(2)}, u32[]{:S(2)}) collective-permute-start(bf16[32,768]{1,0:T(8,128)(2,1)} %get-tuple-element.12), channel_id=1, source_target_pairs={{0,16},{2,18},{4,20},{6,22},{8,24},{10,26},{12,28},{14,30},{16,0},... | collective-permute-start | bytes 147464 | tf_op jit(solution)/shard_map/ppermute | solution.py:223
  43.1 0.0 copy-start.5
  43.1 0.0 copy-start.6
  43.1 10.7 %own_keys.1.own_ref = f32[1024,512]{1,0:T(8,128)} custom-call(s32[1]{0:T(128)S(6)} %copy.26.valid, bf16[2304,512]{1,0:T(8,128)(2,1)} %get-tuple-element.9.q_ref.k_ref.v_ref, bf16[2304,512]{1,0:T(8,128)(2,1)} %get-tuple-element.9.q_ref.k_ref.v_ref, bf16[2304,512]{1,0:T(8,128)(2,1)} %get-tuple-element.9.q_ref.k_ref.v_ref, s32[1,512]{1,0:T(1,128)} %constant.4.clone.pos_ref.ppos_ref), custom_call_target="tpu_custom_call" | custom-call | flops 3221225472 | bytes 3145728 | tf_op jit(solution)/shard_map/own_keys/pallas_call | solution.py:296
  53.8 0.0 copy-done.5
  53.8 0.0 copy-done.6
  53.9 0.6 collective-permute-done.3
  54.5 2.2 %collective-permute-start.4 = (bf16[64,768]{1,0:T(8,128)(2,1)S(1)}, bf16[64,768]{1,0:T(8,128)(2,1)S(1)}, u32[]{:S(2)}, u32[]{:S(2)}) collective-permute-start(bf16[64,768]{1,0:T(8,128)(2,1)S(1)} %pad_maximum_fusion.4), channel_id=1, source_target_pairs={{0,4},{2,6},{4,0},{6,2},{8,12},{10,14},{12,8},{14,10},{16,20},{18,... | collective-permute-start | bytes 294920 | tf_op jit(solution)/shard_map/ppermute | solution.py:223
  56.7 0.0 collective-permute-done.7
  56.7 2.7 %collective-permute-start.8 = (bf16[64,768]{1,0:T(8,128)(2,1)S(1)}, bf16[64,768]{1,0:T(8,128)(2,1)S(1)}, u32[]{:S(2)}, u32[]{:S(2)}) collective-permute-start(bf16[64,768]{1,0:T(8,128)(2,1)S(1)} %pad_maximum_fusion.5), channel_id=1, source_target_pairs={{0,8},{2,10},{4,12},{6,14},{8,0},{10,2},{12,4},{14,6},{16,24},{18,... | collective-permute-start | bytes 294920 | tf_op jit(solution)/shard_map/ppermute | solution.py:223
  59.4 2.8 %collective-permute-done.8 = bf16[64,768]{1,0:T(8,128)(2,1)S(1)} collective-permute-done((bf16[64,768]{1,0:T(8,128)(2,1)S(1)}, bf16[64,768]{1,0:T(8,128)(2,1)S(1)}, u32[]{:S(2)}, u32[]{:S(2)}) %collective-permute-start.8) | collective-permute-done | bytes 98336 | tf_op jit(solution)/shard_map/ppermute | solution.py:223
  62.2 0.3 collective-permute-start.9
  62.5 0.0 collective-permute-done.4
  62.5 2.4 %collective-permute-start.5 = (bf16[128,768]{1,0:T(8,128)(2,1)S(1)}, bf16[128,768]{1,0:T(8,128)(2,1)S(1)}, u32[]{:S(2)}, u32[]{:S(2)}) collective-permute-start(bf16[128,768]{1,0:T(8,128)(2,1)S(1)} %pad_maximum_fusion.2), channel_id=1, source_target_pairs={{0,8},{2,10},{4,12},{6,14},{8,0},{10,2},{12,4},{14,6},{16,24},{18,... | collective-permute-start | bytes 589832 | tf_op jit(solution)/shard_map/ppermute | solution.py:223
  64.9 3.1 %collective-permute-done.9 = bf16[128,768]{1,0:T(8,128)(2,1)S(1)} collective-permute-done((bf16[128,768]{1,0:T(8,128)(2,1)S(1)}, bf16[128,768]{1,0:T(8,128)(2,1)S(1)}, u32[]{:S(2)}, u32[]{:S(2)}) %collective-permute-start.9) | collective-permute-done | bytes 196640 | tf_op jit(solution)/shard_map/ppermute | solution.py:223
  68.0 0.5 collective-permute-start.10
  68.5 2.1 %collective-permute-done.5 = bf16[128,768]{1,0:T(8,128)(2,1)S(1)} collective-permute-done((bf16[128,768]{1,0:T(8,128)(2,1)S(1)}, bf16[128,768]{1,0:T(8,128)(2,1)S(1)}, u32[]{:S(2)}, u32[]{:S(2)}) %collective-permute-start.5) | collective-permute-done | bytes 196640 | tf_op jit(solution)/shard_map/ppermute | solution.py:223
  70.6 1.4 %collective-permute-start.6 = (bf16[256,768]{1,0:T(8,128)(2,1)S(1)}, bf16[256,768]{1,0:T(8,128)(2,1)S(1)}, u32[]{:S(2)}, u32[]{:S(2)}) collective-permute-start(bf16[256,768]{1,0:T(8,128)(2,1)S(1)} %pad_maximum_fusion), channel_id=1, source_target_pairs={{0,16},{2,18},{4,20},{6,22},{8,24},{10,26},{12,28},{14,30},{16,0},... | collective-permute-start | bytes 1179656 | tf_op jit(solution)/shard_map/ppermute | solution.py:223
  72.1 3.7 %collective-permute-done.10 = bf16[256,768]{1,0:T(8,128)(2,1)S(1)} collective-permute-done((bf16[256,768]{1,0:T(8,128)(2,1)S(1)}, bf16[256,768]{1,0:T(8,128)(2,1)S(1)}, u32[]{:S(2)}, u32[]{:S(2)}) %collective-permute-start.10) | collective-permute-done | bytes 393248 | tf_op jit(solution)/shard_map/ppermute | solution.py:223
  75.9 1.0 copy.15
  76.8 7.7 %collective-permute-done.6 = bf16[256,768]{1,0:T(8,128)(2,1)S(1)} collective-permute-done((bf16[256,768]{1,0:T(8,128)(2,1)S(1)}, bf16[256,768]{1,0:T(8,128)(2,1)S(1)}, u32[]{:S(2)}, u32[]{:S(2)}) %collective-permute-start.6) | collective-permute-done | bytes 393248 | tf_op jit(solution)/shard_map/ppermute | solution.py:223
  84.6 0.0 copy-start.3
  84.6 0.0 collective-permute-done.2.rest_1_.rest_3_
  84.6 0.0 copy-start.1
  84.7 0.0 collective-permute-done.1.rest_0_.rest_2_
  84.7 0.0 copy-start.2
  84.7 0.0 collective-permute-done.xp_ref
  84.7 0.0 copy-start.4
  84.7 0.9 copy-done.3
  85.6 0.1 copy-done.1
  85.7 0.2 copy-done.2
  85.8 0.2 copy-done.4
  86.0 25.2 %rest.1 = bf16[512,768]{1,0:T(8,128)(2,1)} custom-call(s32[16]{0:T(128)} %offs.3, s32[1]{0:T(128)S(6)} %copy.26.valid, bf16[512,768]{1,0:T(8,128)(2,1)} %bitcast.19, bf16[512,768]{1,0:T(8,128)(2,1)} %copy-done.4, f32[1,768]{1,0:T(1,128)} %reshape.30.gain_ref, bf16[2304,768]{1,0:T(8,128)(2,1)} %bitcast.16, ...), custom_call_target="tpu_custom_call" | custom-call | flops 4831838208 | bytes 7864320 | tf_op jit(solution)/shard_map/rest/pallas_call | solution.py:310
  111.2 1.7 %copy.17 = bf16[32,1,4,4,768]{4,3,2,0,1:T(4,128)(2,1)S(1)} copy(bf16[32,1,4,4,768]{4,0,2,3,1:T(8,128)(2,1)} %bitcast.21) | data formatting | bytes 1572864 | tf_op jit(solution)/shard_map/transpose | solution.py:343
  113.0 1.1 reshape.35
  (15 shorter events, 0.2 us)
Async XLA Ops:
  0.0 28.0 %all-to-all-start = ((bf16[16,32,768]{2,1,0:T(8,128)(2,1)}), bf16[16,32,768]{2,1,0:T(8,128)(2,1)S(1)}, u32[]{:S(2)}, u32[]{:S(2)}) async-start(bf16[16,32,768]{2,1,0:T(8,128)(2,1)} %bitcast.24), calls=%async_computation | async-start | bytes 1572864 | tf_op jit(solution)/shard_map/all_to_all | solution.py:243
  28.1 0.9 copy-start
  28.1 56.6 %collective-permute-start = (bf16[512,768]{1,0:T(8,128)(2,1)S(1)}, bf16[512,768]{1,0:T(8,128)(2,1)S(1)}, u32[]{:S(2)}, u32[]{:S(2)}) collective-permute-start(bf16[512,768]{1,0:T(8,128)(2,1)S(1)} %bitcast.17), channel_id=1, source_target_pairs={{0,2},{2,0},{4,6},{6,4},{8,10},{10,8},{12,14},{14,12},{16,18},{18,... | collective-permute-start | bytes 2359304 | tf_op jit(solution)/shard_map/ppermute | solution.py:246
  37.2 47.5 %collective-permute-start.2 = (bf16[1536,128]{1,0:T(8,128)(2,1)}, bf16[1536,128]{1,0:T(8,128)(2,1)S(1)}, u32[]{:S(2)}, u32[]{:S(2)}) collective-permute-start(bf16[1536,128]{1,0:T(8,128)(2,1)} %get-tuple-element.10), channel_id=1, source_target_pairs={{0,6},{2,4},{4,2},{6,0},{8,14},{10,12},{12,10},{14,8},{16,22},{18,... | collective-permute-start | bytes 1179656 | tf_op jit(solution)/shard_map/ppermute | solution.py:271
  39.5 45.2 %collective-permute-start.1 = (bf16[1536,128]{1,0:T(8,128)(2,1)}, bf16[1536,128]{1,0:T(8,128)(2,1)S(1)}, u32[]{:S(2)}, u32[]{:S(2)}) collective-permute-start(bf16[1536,128]{1,0:T(8,128)(2,1)} %get-tuple-element.10), channel_id=1, source_target_pairs={{0,4},{2,6},{4,0},{6,2},{8,12},{10,14},{12,8},{14,10},{16,20},{18,... | collective-permute-start | bytes 1179656 | tf_op jit(solution)/shard_map/ppermute | solution.py:271
  39.9 14.6 %collective-permute-start.3 = (bf16[32,768]{1,0:T(8,128)(2,1)}, bf16[32,768]{1,0:T(8,128)(2,1)S(1)}, u32[]{:S(2)}, u32[]{:S(2)}) collective-permute-start(bf16[32,768]{1,0:T(8,128)(2,1)} %get-tuple-element.11), channel_id=1, source_target_pairs={{0,2},{2,0},{4,6},{6,4},{8,10},{10,8},{12,14},{14,12},{16,18},{18,... | collective-permute-start | bytes 147464 | tf_op jit(solution)/shard_map/ppermute | solution.py:223
  40.7 16.0 %collective-permute-start.7 = (bf16[32,768]{1,0:T(8,128)(2,1)}, bf16[32,768]{1,0:T(8,128)(2,1)S(1)}, u32[]{:S(2)}, u32[]{:S(2)}) collective-permute-start(bf16[32,768]{1,0:T(8,128)(2,1)} %get-tuple-element.12), channel_id=1, source_target_pairs={{0,16},{2,18},{4,20},{6,22},{8,24},{10,26},{12,28},{14,30},{16,0},... | collective-permute-start | bytes 147464 | tf_op jit(solution)/shard_map/ppermute | solution.py:223
  43.1 10.7 %copy-start.5 = (bf16[32,768]{1,0:T(8,128)(2,1)S(1)}, bf16[32,768]{1,0:T(8,128)(2,1)}, u32[]{:S(2)}) copy-start(bf16[32,768]{1,0:T(8,128)(2,1)} %get-tuple-element.11) | copy-start | bytes 147460
  43.1 10.7 %copy-start.6 = (bf16[32,768]{1,0:T(8,128)(2,1)S(1)}, bf16[32,768]{1,0:T(8,128)(2,1)}, u32[]{:S(2)}) copy-start(bf16[32,768]{1,0:T(8,128)(2,1)} %get-tuple-element.12) | copy-start | bytes 147460
  54.5 8.0 %collective-permute-start.4 = (bf16[64,768]{1,0:T(8,128)(2,1)S(1)}, bf16[64,768]{1,0:T(8,128)(2,1)S(1)}, u32[]{:S(2)}, u32[]{:S(2)}) collective-permute-start(bf16[64,768]{1,0:T(8,128)(2,1)S(1)} %pad_maximum_fusion.4), channel_id=1, source_target_pairs={{0,4},{2,6},{4,0},{6,2},{8,12},{10,14},{12,8},{14,10},{16,20},{18,... | collective-permute-start | bytes 294920 | tf_op jit(solution)/shard_map/ppermute | solution.py:223
  56.7 5.5 %collective-permute-start.8 = (bf16[64,768]{1,0:T(8,128)(2,1)S(1)}, bf16[64,768]{1,0:T(8,128)(2,1)S(1)}, u32[]{:S(2)}, u32[]{:S(2)}) collective-permute-start(bf16[64,768]{1,0:T(8,128)(2,1)S(1)} %pad_maximum_fusion.5), channel_id=1, source_target_pairs={{0,8},{2,10},{4,12},{6,14},{8,0},{10,2},{12,4},{14,6},{16,24},{18,... | collective-permute-start | bytes 294920 | tf_op jit(solution)/shard_map/ppermute | solution.py:223
  62.2 5.7 %collective-permute-start.9 = (bf16[128,768]{1,0:T(8,128)(2,1)S(1)}, bf16[128,768]{1,0:T(8,128)(2,1)S(1)}, u32[]{:S(2)}, u32[]{:S(2)}) collective-permute-start(bf16[128,768]{1,0:T(8,128)(2,1)S(1)} %pad_maximum_fusion.3), channel_id=1, source_target_pairs={{0,4},{2,6},{4,0},{6,2},{8,12},{10,14},{12,8},{14,10},{16,20},{18,... | collective-permute-start | bytes 589832 | tf_op jit(solution)/shard_map/ppermute | solution.py:223
  62.5 8.1 %collective-permute-start.5 = (bf16[128,768]{1,0:T(8,128)(2,1)S(1)}, bf16[128,768]{1,0:T(8,128)(2,1)S(1)}, u32[]{:S(2)}, u32[]{:S(2)}) collective-permute-start(bf16[128,768]{1,0:T(8,128)(2,1)S(1)} %pad_maximum_fusion.2), channel_id=1, source_target_pairs={{0,8},{2,10},{4,12},{6,14},{8,0},{10,2},{12,4},{14,6},{16,24},{18,... | collective-permute-start | bytes 589832 | tf_op jit(solution)/shard_map/ppermute | solution.py:223
  68.0 7.8 %collective-permute-start.10 = (bf16[256,768]{1,0:T(8,128)(2,1)S(1)}, bf16[256,768]{1,0:T(8,128)(2,1)S(1)}, u32[]{:S(2)}, u32[]{:S(2)}) collective-permute-start(bf16[256,768]{1,0:T(8,128)(2,1)S(1)} %pad_maximum_fusion.1), channel_id=1, source_target_pairs={{0,2},{2,0},{4,6},{6,4},{8,10},{10,8},{12,14},{14,12},{16,18},{18,... | collective-permute-start | bytes 1179656 | tf_op jit(solution)/shard_map/ppermute | solution.py:223
  70.6 14.0 %collective-permute-start.6 = (bf16[256,768]{1,0:T(8,128)(2,1)S(1)}, bf16[256,768]{1,0:T(8,128)(2,1)S(1)}, u32[]{:S(2)}, u32[]{:S(2)}) collective-permute-start(bf16[256,768]{1,0:T(8,128)(2,1)S(1)} %pad_maximum_fusion), channel_id=1, source_target_pairs={{0,16},{2,18},{4,20},{6,22},{8,24},{10,26},{12,28},{14,30},{16,0},... | collective-permute-start | bytes 1179656 | tf_op jit(solution)/shard_map/ppermute | solution.py:223
  84.6 0.9 copy-start.3
  84.6 1.0 copy-start.1
  84.7 1.2 %copy-start.2 = (bf16[1536,128]{1,0:T(8,128)(2,1)}, bf16[1536,128]{1,0:T(8,128)(2,1)S(1)}, u32[]{:S(2)}) copy-start(bf16[1536,128]{1,0:T(8,128)(2,1)S(1)} %collective-permute-done.1.rest_0_.rest_2_) | copy-start | bytes 1179652
  84.7 1.4 %copy-start.4 = (bf16[512,768]{1,0:T(8,128)(2,1)}, bf16[512,768]{1,0:T(8,128)(2,1)S(1)}, u32[]{:S(2)}) copy-start(bf16[512,768]{1,0:T(8,128)(2,1)S(1)} %collective-permute-done.xp_ref) | copy-start | bytes 2359300
where the time goes:
time: 115 us; the launch traced here: 114 us
  Pallas kernels  44.1 us (38%)
  waiting for transfers between devices  30.4 us (26%)
  starting transfers between devices  24.4 us (21%)
  local copies, waits for them, and re-layouts  14.2 us (12%)
    pallas_call x1, Pallas kernels, body(): pl.pallas_call(functools.partial(rest_kernel, heads, scale, per_step, far...  25.2 us
    ppermute x8, waiting for transfers between devices, doubled(): return jnp.concatenate([rows, lax.ppermute(rows, 'seq', pairs)], axis=0)  20 us
    ppermute x8, starting transfers between devices, doubled(): return jnp.concatenate([rows, lax.ppermute(rows, 'seq', pairs)], axis=0)  12.8 us
    pallas_call x1, Pallas kernels, body(): pl.pallas_call(functools.partial(own_kernel, scale, per_step, size), grid...  10.7 us
    all_to_all x1, waiting for transfers between devices, body(): lax.all_to_all(pieces, 'seq', split_axis=0, concat_axis=0, tiled=True)  10.4 us
    all_to_all x1, starting transfers between devices, body(): lax.all_to_all(pieces, 'seq', split_axis=0, concat_axis=0, tiled=True)  8.34 us
    pallas_call x1, Pallas kernels, body(): pl.pallas_call(functools.partial(project_kernel, heads), out_shape=(jax.S...  8.2 us
    unnamed x22, local copies, waits for them, and re-layouts  7.43 us
  transfers between devices with their start and end apart: 12, of which 7 were waited for; matrix products, arithmetic and copies ran while one was open for 9% of the time, Pallas kernels for 17%

commit v1 on v0

--- a/solution.py
+++ b/solution.py
@@ -223,7 +223,7 @@
     return jnp.concatenate([rows, lax.ppermute(rows, "seq", pairs)], axis=0)
 
 
-def body(tile_embed, valid_tiles, offsets, norm_gain, w_qkv, sub_gain, w_out):
+def gathered_body(tile_embed, valid_tiles, offsets, norm_gain, w_qkv, sub_gain, w_out):
     devices = lax.axis_size("seq")
     me = lax.axis_index("seq")
     rows, width = tile_embed.shape
@@ -344,7 +344,480 @@
     )
 
 
+def flip(number, mask):
+    for bit in range(mask.bit_length()):
+        if mask >> bit & 1:
+            number = number + (1 << bit) * (1 - 2 * ((number // (1 << bit)) % 2))
+    return number
+
+
+def to(device):
+    return {"seq": device}
+
+
+def remote(src, dst, send, recv, device):
+    return pltpu.make_async_remote_copy(
+        src_ref=src, dst_ref=dst, send_sem=send, recv_sem=recv,
+        device_id=to(device), device_id_type=pl.DeviceIdType.MESH,
+    )
+
+
+def split_rows(total, top):
+    lanes = total.shape[1]
+    spot = lax.broadcasted_iota(jnp.int32, (AUG, lanes), 0)
+    rounded = lambda a: a.astype(jnp.bfloat16).astype(jnp.float32)
+    total_high = rounded(total)
+    top_high = rounded(top)
+    top_mid = rounded(top - top_high)
+    parts = [total_high, total - total_high, top_high, top_mid, top - top_high - top_mid]
+    rows = jnp.zeros((AUG, lanes), jnp.float32)
+    for i, part in enumerate(parts):
+        rows = jnp.where(spot == i, part, rows)
+    return rows
+
+
+def layer_kernel(
+    heads, devices, scale,
+    offs, valid, x_hbm, gain_ref, w_hbm, subgain_ref, wout_hbm,
+    out_ref,
+    xr, normed, xown, w_v, w_t, wout_v, qa, ka, va, acc, att,
+    mtx, mrx, mres, mret, fmsg, frx, fres, fret,
+    s1, r1, s2, r2, ms, mr, ns, nr, fs, fr, gs, gr, ws,
+):
+    rows, width = out_ref.shape
+    size = width // heads
+    half = devices // 2
+    each = rows // devices
+    lanes = rows // MIDDLE_DILATION
+    few = rows // FAR_DILATION
+    group = mrx.shape[0]
+    per_group = heads // group
+    pad = size + AUG
+    mid_chunk = rows // 2
+    me = lax.axis_index("seq")
+    par = me % 2
+    pair = me // 2
+    partner = me + 1 - 2 * par
+    seat = me % group
+    base = me - seat
+
+    load_w = pltpu.make_async_copy(w_hbm, w_v, ws.at[0])
+    load_w.start()
+    load_wout = pltpu.make_async_copy(wout_hbm, wout_v, ws.at[1])
+    load_wout.start()
+    own_block = pltpu.make_async_copy(x_hbm.at[pair], xr.at[0, pair], ws.at[2])
+    own_block.start()
+
+    barrier = pltpu.get_barrier_semaphore()
+    for d in range(1, devices):
+        pl.semaphore_signal(
+            barrier, inc=1, device_id=to(flip(me, d)), device_id_type=pl.DeviceIdType.MESH
+        )
+    pl.semaphore_wait(barrier, devices - 1)
+
+    def first(j):
+        other = flip(pair, j)
+        return remote(
+            x_hbm.at[other], xr.at[0, pair], s1.at[j], r1.at[pair], 2 * other + par
+        )
+
+    def first_arrival(j):
+        other = flip(pair, j)
+        return remote(
+            x_hbm.at[other], xr.at[0, other], s1.at[j], r1.at[other], 2 * other + par
+        )
+
+    def second(k):
+        return remote(xr.at[0, k], xr.at[1, k], s2.at[k], r2.at[k], partner)
+
+    for j in range(1, half):
+        first(j).start()
+    own_block.wait()
+    second(pair).start()
+
+    column = lax.broadcasted_iota(jnp.int32, (1, rows), 1)
+    block = column // few
+    side = (block // half + par) % 2
+    phase = (block % 4) * 4 + ((block % half) // 4) * 2 + side
+    place = (column % few) * FAR_DILATION + phase
+    unit = aug_rows(jnp.ones((1, rows), jnp.float32), rows)
+    alive = []
+    for device in (me, partner):
+        alive.append((place + device * rows < valid[0]))
+    weights = [jnp.where(a, 1.0, 0.0) for a in alive]
+    biases = [aug_rows(jnp.where(a, 0.0, NEGATIVE), rows) for a in alive]
+    weight_rows = [aug_rows(a, rows) for a in weights]
+
+    @pl.loop(0, heads)
+    def _(h):
+        qa[h, size:, :] = unit
+        for m in range(2):
+            ka[h, size:, m * rows : (m + 1) * rows] = biases[m]
+            va[h, size:, m * rows : (m + 1) * rows] = weight_rows[m]
+
+    load_w.wait()
+
+    @pl.loop(0, w_v.shape[1] // 256)
+    def _(i):
+        cols = pl.ds(pl.multiple_of(i * 256, 256), 256)
+        w_t[cols, :] = w_v[:, cols].T
+
+    gain = gain_ref[...].reshape(1, width)
+
+    def norm_block(side_index, k):
+        spot = side_index * half + (k % 2) * (half // 2) + k // 2
+        at = pl.ds(pl.multiple_of(spot * each, each), each)
+        mine = xr[side_index, k, par]
+        xown[at, :] = mine
+        normed[0, at, :] = layer_norm_rows(mine.astype(jnp.float32), gain).astype(jnp.bfloat16)
+        theirs = xr[side_index, k, 1 - par]
+        normed[1, at, :] = layer_norm_rows(theirs.astype(jnp.float32), gain).astype(jnp.bfloat16)
+
+    norm_block(0, pair)
+    for j in range(1, half):
+        k = flip(pair, j)
+        first_arrival(j).wait_recv()
+        second(k).start()
+        norm_block(0, k)
+
+    def project(c):
+        at = slice(c * mid_chunk, (c + 1) * mid_chunk)
+        for m in range(2):
+            tokens = normed[m, at, :]
+            where = slice(m * rows + c * mid_chunk, m * rows + (c + 1) * mid_chunk)
+            for part in range(3):
+                if m == 1 and part == 0:
+                    continue
+                for g in range(2):
+                    count = heads // 2
+                    first_row = part * width + g * count * size
+                    result = lax.dot_general(
+                        w_t[first_row : first_row + count * size, :], tokens,
+                        (((1,), (1,)), ((), ())), preferred_element_type=jnp.float32,
+                    )
+                    if part == 0:
+                        result = result * scale
+                    if part == 2:
+                        result = result * weights[m][:, at]
+                    result = result.astype(jnp.bfloat16)
+                    dst = (qa, ka, va)[part]
+                    for i in range(count):
+                        dst[g * count + i, :size, where] = result[i * size : (i + 1) * size]
+
+    project(0)
+    for j in range(half):
+        k = flip(pair, j)
+        second(k).wait_recv()
+        norm_block(1, k)
+    project(1)
+
+    pick_row = lax.broadcasted_iota(jnp.int32, (3 * lanes, lanes), 0)
+    pick_col = lax.broadcasted_iota(jnp.int32, (1, lanes), 1)
+    source = jnp.where(
+        pick_col < 3 * few, (pick_col // few) * lanes + pick_col % few, -devices * rows
+    )
+
+    def head_spot(h):
+        turn = offs[h] % FAR_DILATION
+        where = ((turn + par) % 2) * 2 + (turn // 2) % 2
+        return turn, where
+
+    all_rows = lax.broadcasted_iota(jnp.int32, (rows, lanes), 0)
+    ahead = all_rows - lax.broadcasted_iota(jnp.int32, (rows, lanes), 1)
+
+    @pl.loop(0, heads)
+    def _(h):
+        turn, where = head_spot(h)
+        choose = jnp.where(ahead == where * lanes, 1.0, 0.0).astype(jnp.bfloat16)
+        chosen = jnp.dot(
+            jnp.concatenate([qa[h, :size, :], ka[h, :size, :rows], va[h, :size, :rows]], axis=0),
+            choose, preferred_element_type=jnp.float32,
+        ).astype(jnp.bfloat16)
+        mtx[h // per_group, h % per_group] = chosen
+        pick = jnp.where(pick_row == source + (turn // 4) * few, 1.0, 0.0).astype(jnp.bfloat16)
+        pieces = [chosen[i * size : (i + 1) * size] for i in range(3)]
+        fmsg[h] = jnp.dot(
+            jnp.concatenate(pieces, axis=1), pick, preferred_element_type=jnp.float32
+        ).astype(jnp.bfloat16)
+
+    def mid_send(j):
+        other = flip(seat, j)
+        return remote(mtx.at[other], mrx.at[seat], ms.at[j], mr.at[seat], base + other)
+
+    def mid_arrival(j):
+        other = flip(seat, j)
+        return remote(mtx.at[other], mrx.at[other], ms.at[j], mr.at[other], base + other)
+
+    def far_send(j):
+        other = flip(me, j)
+        return remote(fmsg.at[other], frx.at[me], fs.at[j], fr.at[me], other)
+
+    def far_arrival(j):
+        other = flip(me, j)
+        return remote(fmsg.at[other], frx.at[other], fs.at[j], fr.at[other], other)
+
+    for j in range(1, devices):
+        far_send(j).start()
+    for j in range(1, group):
+        mid_send(j).start()
+    mrx[seat] = mtx[seat]
+    frx[me] = fmsg[me]
+
+    def attend(keys, queries, values):
+        scores = scores_of(keys, queries)
+        top = jnp.max(scores, axis=0, keepdims=True)
+        p = jnp.exp2(scores - top).astype(jnp.bfloat16)
+        return jnp.dot(values, p, preferred_element_type=jnp.float32), top
+
+    def near(h):
+        for n in range(2):
+            cols = slice(n * mid_chunk, (n + 1) * mid_chunk)
+            got, top = attend(ka[h], qa[h, :, cols], va[h])
+            acc[h, :, cols] = got
+            acc[h, size + 1 : size + 2, cols] = top
+
+    first_heads = heads // 2
+
+    @pl.loop(0, first_heads)
+    def _(h):
+        near(h)
+
+    for j in range(1, group):
+        mid_arrival(j).wait_recv()
+
+    mid_lane = lax.broadcasted_iota(jnp.int32, (1, group * lanes), 1)
+    mid_place = (
+        (base + mid_lane // lanes) * rows
+        + (mid_lane % few) * FAR_DILATION
+        + ((mid_lane % lanes) // few) * MIDDLE_DILATION
+    )
+
+    @pl.loop(0, per_group)
+    def _(i):
+        quarter = offs[seat * per_group + i] % MIDDLE_DILATION
+        live = mid_place + quarter < valid[0]
+        joined = [
+            jnp.concatenate(
+                [mrx[g, i, p * size : (p + 1) * size, :] for g in range(group)], axis=1
+            )
+            for p in range(3)
+        ]
+        queries = jnp.concatenate(
+            [joined[0], aug_rows(jnp.ones((1, group * lanes), jnp.float32), group * lanes)], axis=0
+        )
+        keys = jnp.concatenate(
+            [joined[1], aug_rows(jnp.where(live, 0.0, NEGATIVE), group * lanes)], axis=0
+        )
+        values = jnp.concatenate(
+            [joined[2], aug_rows(jnp.where(live, 1.0, 0.0), group * lanes)], axis=0
+        )
+        for n in range(2):
+            wide = group * lanes // 2
+            got, top = attend(keys, queries[:, n * wide : (n + 1) * wide], values)
+            sent = jnp.concatenate(
+                [got[:size], split_rows(got[size : size + 1], top)], axis=0
+            ).astype(jnp.bfloat16)
+            for g in range(group // 2):
+                mres[n * (group // 2) + g, i] = sent[:, g * lanes : (g + 1) * lanes]
+
+    def mid_return(j):
+        other = flip(seat, j)
+        return remote(mres.at[other], mret.at[seat], ns.at[j], nr.at[seat], base + other)
+
+    def mid_returned(j):
+        other = flip(seat, j)
+        return remote(mres.at[other], mret.at[other], ns.at[j], nr.at[other], base + other)
+
+    for j in range(1, group):
+        mid_return(j).start()
+    mret[seat] = mres[seat]
+
+    for j in range(1, devices):
+        far_arrival(j).wait_recv()
+
+    my_turn = offs[me] % FAR_DILATION
+    turned = [frx[d].T for d in range(devices)]
+    far_q, far_k, far_v = (
+        jnp.concatenate([t[p * few : (p + 1) * few] for t in turned], axis=0) for p in range(3)
+    )
+    far_row = lax.broadcasted_iota(jnp.int32, (devices * few, 1), 0)
+    far_live = far_row * FAR_DILATION + my_turn < valid[0]
+    far_size = devices * few // 2
+    sums = lax.broadcasted_iota(jnp.int32, (devices * few, AUG), 1) == 0
+    for n in range(2):
+        scores = lax.dot_general(
+            far_k, far_q[n * far_size : (n + 1) * far_size], (((1,), (1,)), ((), ())),
+            preferred_element_type=jnp.float32,
+        )
+        scores = jnp.where(far_live, scores, NEGATIVE)
+        top = jnp.max(scores, axis=0, keepdims=True)
+        p = jnp.exp2(scores - top).astype(jnp.bfloat16)
+        count = jnp.where(far_live, jnp.where(far_row // far_size == n, 2.0, 1.0), 0.0)
+        numer = lax.dot_general(
+            (far_v.astype(jnp.float32) * count).astype(jnp.bfloat16), p,
+            (((0,), (0,)), ((), ())), preferred_element_type=jnp.float32,
+        )
+        total = lax.dot_general(
+            jnp.where(sums, count, 0.0).astype(jnp.bfloat16), p,
+            (((0,), (0,)), ((), ())), preferred_element_type=jnp.float32,
+        )
+        sent = jnp.concatenate(
+            [numer, split_rows(total[:1], top),
+             jnp.zeros((lanes - pad, far_size), jnp.float32)], axis=0,
+        ).T.astype(jnp.bfloat16)
+        for d in range(devices // 2):
+            fres[n * (devices // 2) + d] = sent[d * few : (d + 1) * few]
+
+    def far_return(j):
+        other = flip(me, j)
+        return remote(fres.at[other], fret.at[me], gs.at[j], gr.at[me], other)
+
+    def far_returned(j):
+        other = flip(me, j)
+        return remote(fres.at[other], fret.at[other], gs.at[j], gr.at[other], other)
+
+    for j in range(1, devices):
+        far_return(j).start()
+    fret[me] = fres[me]
+
+    @pl.loop(first_heads, heads)
+    def _(h):
+        near(h)
+
+    for j in range(1, group):
+        mid_returned(j).wait_recv()
+    for j in range(1, devices):
+        far_returned(j).wait_recv()
+
+    few_row = lax.broadcasted_iota(jnp.int32, (few, rows), 0)
+
+    @pl.loop(0, heads)
+    def _(h):
+        turn, _ = head_spot(h)
+        in_mid = phase % MIDDLE_DILATION == turn % MIDDLE_DILATION
+        in_far = phase == turn
+        mid = mret[h // per_group, h % per_group].astype(jnp.float32)
+        mid = jnp.concatenate([mid] * (rows // lanes), axis=1)
+        spread = jnp.where(in_far & (column % few == few_row), 1.0, 0.0).astype(jnp.bfloat16)
+        far = lax.dot_general(
+            fret[h], spread, (((0,), (0,)), ((), ())), preferred_element_type=jnp.float32
+        )
+        near_top = acc[h, size + 1 : size + 2, :]
+
+        def stats(a):
+            return (
+                a[size : size + 1] + a[size + 1 : size + 2],
+                a[size + 2 : size + 3] + a[size + 3 : size + 4] + a[size + 4 : size + 5],
+            )
+
+        mid_total, mid_top = stats(mid)
+        far_total, far_top = stats(far)
+        top = jnp.maximum(
+            near_top,
+            jnp.maximum(jnp.where(in_mid, mid_top, NEGATIVE), jnp.where(in_far, far_top, NEGATIVE)),
+        )
+        near_by = jnp.exp2(near_top - top)
+        mid_by = jnp.where(in_mid, jnp.exp2(jnp.where(in_mid, mid_top, NEGATIVE) - top), 0.0)
+        far_by = jnp.where(in_far, jnp.exp2(jnp.where(in_far, far_top, NEGATIVE) - top), 0.0)
+        den = near_by * acc[h, size : size + 1, :] + mid_by * mid_total + far_by * far_total
+        num = near_by * acc[h, :size, :] + mid_by * mid[:size] + far_by * far[:size]
+        att[pl.ds(pl.multiple_of(h * size, AUG), size), :] = (
+            num / jnp.maximum(den, 1.0)
+        ).astype(jnp.bfloat16)
+
+    load_wout.wait()
+    subgain = subgain_ref[...].reshape(1, width)
+    for c in range(2):
+        at = slice(c * mid_chunk, (c + 1) * mid_chunk)
+        target = lax.broadcasted_iota(jnp.int32, (mid_chunk, 1), 0) + c * mid_chunk
+        order = jnp.where(place == target, 1.0, 0.0).astype(jnp.bfloat16)
+        attended = lax.dot_general(
+            order, att[...], (((1,), (1,)), ((), ())), preferred_element_type=jnp.float32
+        )
+        residual = jnp.dot(order, xown[...], preferred_element_type=jnp.float32)
+        sub_normed = layer_norm_rows(attended, subgain).astype(jnp.bfloat16)
+        out_ref[at, :] = (
+            residual + jnp.dot(sub_normed, wout_v[...], preferred_element_type=jnp.float32)
+        ).astype(jnp.bfloat16)
+
+    for j in range(1, half):
+        first(j).wait_send()
+    for j in range(half):
+        second(flip(pair, j)).wait_send()
+    for j in range(1, group):
+        mid_send(j).wait_send()
+        mid_return(j).wait_send()
+    for j in range(1, devices):
+        far_send(j).wait_send()
+        far_return(j).wait_send()
+
+
+def exchanged_body(tile_embed, valid_tiles, offsets, norm_gain, w_qkv, sub_gain, w_out):
+    devices = lax.axis_size("seq")
+    rows, width = tile_embed.shape
+    heads = offsets.shape[0]
+    size = width // heads
+    pad = size + AUG
+    half = devices // 2
+    each = rows // devices
+    lanes = rows // MIDDLE_DILATION
+    few = rows // FAR_DILATION
+    group = max(4, devices // 16)
+    per_group = heads // group
+    scale = float(size) ** -0.5 * LOG2E
+    bf16 = lambda *shape: pltpu.VMEM(shape, jnp.bfloat16)
+    vmem = pl.BlockSpec(memory_space=pltpu.VMEM)
+    smem = pl.BlockSpec(memory_space=pltpu.SMEM)
+    anywhere = pl.BlockSpec(memory_space=pl.ANY)
+    sems = lambda n: pltpu.SemaphoreType.DMA((n,))
+    return pl.pallas_call(
+        functools.partial(layer_kernel, heads, devices, scale),
+        out_shape=jax.ShapeDtypeStruct((rows, width), jnp.bfloat16),
+        in_specs=[smem, smem, anywhere, vmem, anywhere, vmem, anywhere],
+        out_specs=vmem,
+        scratch_shapes=[
+            bf16(2, half, 2, each, width),
+            bf16(2, rows, width),
+            bf16(rows, width),
+            bf16(*w_qkv.shape),
+            bf16(*w_qkv.shape[::-1]),
+            bf16(*w_out.shape),
+            bf16(heads, pad, rows),
+            bf16(heads, pad, 2 * rows),
+            bf16(heads, pad, 2 * rows),
+            pltpu.VMEM((heads, pad, rows), jnp.float32),
+            bf16(width, rows),
+            bf16(group, per_group, 3 * size, lanes),
+            bf16(group, per_group, 3 * size, lanes),
+            bf16(group, per_group, pad, lanes),
+            bf16(group, per_group, pad, lanes),
+            bf16(heads, size, lanes),
+            bf16(devices, size, lanes),
+            bf16(devices, few, lanes),
+            bf16(heads, few, lanes),
+            sems(half), sems(half), sems(half), sems(half),
+            sems(group), sems(group), sems(group), sems(group),
+            sems(devices), sems(devices), sems(devices), sems(devices),
+            sems(3),
+        ],
+        compiler_params=pltpu.CompilerParams(
+            vmem_limit_bytes=VMEM_LIMIT, collective_id=0, has_side_effects=True
+        ),
+        name="layer",
+    )(
+        offsets, valid_tiles, tile_embed.reshape(half, 2, each, width), norm_gain, w_qkv,
+        sub_gain, w_out,
+    )
+
+
 def solution(mesh):
+    devices = mesh.shape["seq"]
+
+    def body(tile_embed, valid_tiles, offsets, *rest):
+        fits = devices == offsets.shape[0] == FAR_DILATION and tile_embed.shape[0] % (16 * devices) == 0
+        run = exchanged_body if fits else gathered_body
+        return run(tile_embed, valid_tiles, offsets, *rest)
+
     return jax.shard_map(
         body,
         mesh=mesh,

time: 115 us -> 76.7 us (0.67)
  waiting for transfers between devices: 30.4 us -> 0 us
  Pallas kernels: 44.1 us -> 73.7 us
  starting transfers between devices: 24.4 us -> 0 us
  local copies, waits for them, and re-layouts: 14.2 us -> 2.06 us
    pallas_call x3 -> x1, Pallas kernels: 44.1 us -> 73.7 us  [exchanged_body(): pl.pallas_call(functools.partial(layer_kernel, heads, devices, scale), ou...]
    ppermute x11 -> x0, waiting for transfers between devices: 20 us -> none  [the longest x8 20 us: doubled(): return jnp.concatenate([rows, lax.ppermute(rows, 'seq', pairs)], axis=0)]
    ppermute x11 -> x0, starting transfers between devices: 16.1 us -> none  [the longest x8 12.8 us: doubled(): return jnp.concatenate([rows, lax.ppermute(rows, 'seq', pairs)], axis=0)]
    all_to_all x1 -> x0, waiting for transfers between devices: 10.4 us -> none  [body(): lax.all_to_all(pieces, 'seq', split_axis=0, concat_axis=0, tiled=True)]
    all_to_all x1 -> x0, starting transfers between devices: 8.34 us -> none  [body(): lax.all_to_all(pieces, 'seq', split_axis=0, concat_axis=0, tiled=True)]
    unnamed x22 -> x1, local copies, waits for them, and re-layouts: 7.43 us -> 2.06 us
    reshape x4 -> x0, local copies, waits for them, and re-layouts: 4.91 us -> none  [the longest x1 1.6 us: body(): sub_gain.reshape(width, 1)]
    transpose x2 -> x0, local copies, waits for them, and re-layouts: 1.8 us -> none  [the longest x1 1.74 us: body(): out.reshape(4, 4, groups, each, width).transpose(3, 2, 1, 0, 4)]
  transfers between devices with their start and end apart: 12 -> 0, of which waited for: 7 -> 0; matrix products, arithmetic and copies ran while one was open for 9% -> 0% of each run, Pallas kernels for 17% -> 0%
where the time goes in v1:
time: 76.7 us; the launch traced here: 76.5 us
  Pallas kernels  73.7 us (96%)
  local copies, waits for them, and re-layouts  2.06 us (3%)
    pallas_call x1, Pallas kernels, exchanged_body(): pl.pallas_call(functools.partial(layer_kernel, heads, devices, scale), ou...  73.7 us
    unnamed x1, local copies, waits for them, and re-layouts  2.06 us

profile of v1, /device:TPU:0, one launch (start us, length us, event | category | flops | bytes accessed | tf_op | source)
XLA Modules:
  0.0 76.5 jit_solution(17592237097937472752)
XLA Ops:
  0.7 73.7 %layer.1 = bf16[512,768]{1,0:T(8,128)(2,1)} custom-call(s32[16]{0:T(128)} %offs.1, s32[1]{0:T(128)S(6)} %copy.9.valid, bf16[8,2,32,768]{3,2,1,0:T(8,128)(2,1)} %bitcast.1, f32[768]{0:T(1024)} %gain_ref.1, bf16[768,2304]{1,0:T(8,128)(2,1)} %w_hbm.1, f32[768]{0:T(1024)} %subgain_ref.1, bf16[768,768]{1,0:T(8,128)(2,1)} %wout_hbm.1), custom_call_target="tpu_custom_call" | custom-call | tf_op jit(solution)/shard_map/layer/pallas_call | solution.py:773
  74.4 2.1 %copy.10 = bf16[512,768]{1,0:T(8,128)(2,1)} copy(bf16[512,768]{1,0:T(8,128)(2,1)} %layer.1) | data formatting | bytes 1572864

commit v2 on v0

--- a/solution.py
+++ b/solution.py
@@ -223,7 +223,7 @@
     return jnp.concatenate([rows, lax.ppermute(rows, "seq", pairs)], axis=0)
 
 
-def body(tile_embed, valid_tiles, offsets, norm_gain, w_qkv, sub_gain, w_out):
+def gathered_body(tile_embed, valid_tiles, offsets, norm_gain, w_qkv, sub_gain, w_out):
     devices = lax.axis_size("seq")
     me = lax.axis_index("seq")
     rows, width = tile_embed.shape
@@ -344,7 +344,558 @@
     )
 
 
+def flip(number, mask):
+    for bit in range(mask.bit_length()):
+        if mask >> bit & 1:
+            number = number + (1 << bit) * (1 - 2 * ((number // (1 << bit)) % 2))
+    return number
+
+
+def to(device):
+    return {"seq": device}
+
+
+def remote(src, dst, send, recv, device):
+    return pltpu.make_async_remote_copy(
+        src_ref=src, dst_ref=dst, send_sem=send, recv_sem=recv,
+        device_id=to(device), device_id_type=pl.DeviceIdType.MESH,
+    )
+
+
+def split_rows(total, top):
+    lanes = total.shape[1]
+    spot = lax.broadcasted_iota(jnp.int32, (AUG, lanes), 0)
+    rounded = lambda a: a.astype(jnp.bfloat16).astype(jnp.float32)
+    total_high = rounded(total)
+    top_high = rounded(top)
+    top_mid = rounded(top - top_high)
+    parts = [total_high, total - total_high, top_high, top_mid, top - top_high - top_mid]
+    rows = jnp.zeros((AUG, lanes), jnp.float32)
+    for i, part in enumerate(parts):
+        rows = jnp.where(spot == i, part, rows)
+    return rows
+
+
+def layer_kernel(
+    heads, devices, scale,
+    offs, valid, x_hbm, gain_ref, w_hbm, subgain_ref, wout_hbm,
+    out_ref,
+    xr, normed, w_v, w_t, wout_v, qkv, acc, att, bank, s_even, s_odd, t_even, t_odd,
+    mq, mqrx, mk, mv, mloc, mres, mret, fmsg, frx, fq, fk, fv, fres, fret,
+    s1, r1, s2, r2, s3, r3, ms, mr, ns, nr, fs, fr, gs, gr, ws,
+):
+    rows, width = out_ref.shape
+    size = width // heads
+    half = devices // 2
+    each = rows // devices
+    lanes = rows // MIDDLE_DILATION
+    few = rows // FAR_DILATION
+    pad = size + AUG
+    wide = rows // 2
+    batch = 4
+    handle_at = heads // 4 - 1
+    batches = heads // batch
+    me = lax.axis_index("seq")
+    par = me % 2
+    pair = me // 2
+    partner = flip(me, 1)
+    across = flip(me, 2)
+
+    seat_of = lambda k: (k % 2) * (half // 2) + k // 2
+    load_w = pltpu.make_async_copy(w_hbm, w_v, ws.at[0])
+    load_w.start()
+    load_wout = pltpu.make_async_copy(wout_hbm, wout_v, ws.at[1])
+    load_wout.start()
+    own_block = pltpu.make_async_copy(x_hbm.at[pair], xr.at[0, :, seat_of(pair)], ws.at[2])
+    own_block.start()
+
+    barrier = pltpu.get_barrier_semaphore()
+    for d in range(1, devices):
+        pl.semaphore_signal(
+            barrier, inc=1, device_id=to(flip(me, d)), device_id_type=pl.DeviceIdType.MESH
+        )
+    pl.semaphore_wait(barrier, devices - 1)
+
+    def first(j):
+        other = flip(pair, j)
+        return remote(
+            x_hbm.at[other], xr.at[0, :, seat_of(pair)], s1.at[j], r1.at[pair], 2 * other + par
+        )
+
+    def first_arrival(j):
+        other = flip(pair, j)
+        return remote(
+            x_hbm.at[other], xr.at[0, :, seat_of(other)], s1.at[j], r1.at[other], 2 * other + par
+        )
+
+    def forward(j, member, arrives, send, recv):
+        k = flip(pair, j)
+        return remote(
+            xr.at[0, member, seat_of(k)], xr.at[1, arrives, seat_of(k)],
+            send.at[j], recv.at[k], partner,
+        )
+
+    def urgent(j):
+        return forward(j, 1 - par, 1 - par, s2, r2)
+
+    def urgent_arrival(j):
+        return forward(j, 1 - par, par, s2, r2)
+
+    def later(j):
+        return forward(j, par, par, s3, r3)
+
+    def later_arrival(j):
+        return forward(j, par, 1 - par, s3, r3)
+
+    for j in range(1, half):
+        first(j).start()
+    own_block.wait()
+    urgent(0).start()
+    later(0).start()
+
+    column = lax.broadcasted_iota(jnp.int32, (1, rows), 1)
+    block = column // few
+    side = (block // half + par) % 2
+    phase = (block % 4) * 4 + ((block % half) // 4) * 2 + side
+    place = (column % few) * FAR_DILATION + phase
+    unit = aug_rows(jnp.ones((1, rows), jnp.float32), rows)
+    alive = [place + device * rows < valid[0] for device in (me, partner)]
+    biases = [aug_rows(jnp.where(a, 0.0, NEGATIVE), rows) for a in alive]
+    weight_rows = [aug_rows(jnp.where(a, 1.0, 0.0), rows) for a in alive]
+
+    @pl.loop(0, heads)
+    def _(h):
+        qkv[h, size:, :rows] = unit
+        for m in range(2):
+            qkv[heads + h, size:, m * rows : (m + 1) * rows] = biases[m]
+            qkv[2 * heads + h, size:, m * rows : (m + 1) * rows] = weight_rows[m]
+
+    bank_row = lax.broadcasted_iota(jnp.int32, (3 * lanes, 1), 0)
+    bank_col = lax.broadcasted_iota(jnp.int32, (1, batch * lanes), 1)
+    spot = bank_col % lanes
+    source = jnp.where(
+        spot < 3 * few, (spot // few) * lanes + (bank_col // lanes) * few + spot % few, -1
+    )
+    bank[...] = jnp.where(bank_row == source, 1.0, 0.0).astype(jnp.bfloat16)
+
+    load_w.wait()
+
+    @pl.loop(0, w_v.shape[1] // 256)
+    def _(i):
+        cols = pl.ds(pl.multiple_of(i * 256, 256), 256)
+        w_t[cols, :] = w_v[:, cols].T
+
+    gain = gain_ref[...].reshape(1, width)
+
+    def norm(m, c, first_seat, seats):
+        count = seats * each
+        piece = xr[c, par + m - 2 * par * m, pl.ds(first_seat, seats)]
+        piece = piece.reshape(count, width).astype(jnp.float32)
+        at = pl.ds(pl.multiple_of(c * wide + first_seat * each, count), count)
+        normed[m, at, :] = layer_norm_rows(piece, gain).astype(jnp.bfloat16)
+
+    quarter_seats = half // 4
+    zone = (pair // 2) // quarter_seats
+    for g in range(2):
+        for j in range(max(1, g * half // 2), (g + 1) * half // 2):
+            first_arrival(j).wait_recv()
+            urgent(j).start()
+            if g == 0:
+                later(j).start()
+        z = zone if g == 0 else 1 - zone
+
+        @pl.loop(0, 4)
+        def _(t):
+            norm(t // 2, 0, (t % 2) * (half // 2) + z * quarter_seats, quarter_seats)
+
+    for j in range(half // 2, half):
+        later(j).start()
+
+    def project(c, start, stop):
+        @pl.loop(start, stop)
+        def _(t):
+            m = t // 3
+            part = t - 2 * m
+            at = slice(c * wide, (c + 1) * wide)
+            device = me + m * (partner - me)
+            weight = jnp.where(place[:, at] + device * rows < valid[0], 1.0, 0.0)
+            part_row = jnp.zeros((1, wide), jnp.int32) + part
+            factor = jnp.where(part_row == 0, scale, jnp.where(part_row == 2, weight, 1.0))
+            result = lax.dot_general(
+                w_t[pl.ds(pl.multiple_of(part * width, width), width), :], normed[m, at, :],
+                (((1,), (1,)), ((), ())), preferred_element_type=jnp.float32,
+            )
+            result = (result * factor).astype(jnp.bfloat16)
+            where = pl.ds(pl.multiple_of(m * rows + c * wide, wide), wide)
+            for i in range(heads):
+                qkv[part * heads + i, :size, where] = result[i * size : (i + 1) * size]
+
+    project(0, 0, 5)
+    for j in range(half):
+        urgent_arrival(j).wait_recv()
+
+    @pl.loop(0, 4)
+    def _(t):
+        norm(0, 1, t * quarter_seats, quarter_seats)
+
+    project(1, 0, 3)
+
+    def head_turn(h):
+        turn = offs[h] % FAR_DILATION
+        return turn, ((turn + par) % 2) * 2 + (turn // 2) % 2
+
+    ones = jnp.zeros((1, lanes), jnp.int32)
+
+    def chosen(row, shift, where):
+        total = None
+        for b in range(MIDDLE_DILATION):
+            by = jnp.where(ones + where == b, 1.0, 0.0).astype(jnp.bfloat16)
+            piece = qkv[row, :size, shift + b * lanes : shift + (b + 1) * lanes] * by
+            total = piece if total is None else total + piece
+        return total
+
+    @pl.loop(0, batches)
+    def _(c):
+        turns = [head_turn(c * batch + i) for i in range(batch)]
+        stacked = []
+        for i in range(batch):
+            h = c * batch + i
+            pieces = [chosen(p * heads + h, 0, turns[i][1]) for p in range(3)]
+            mq[c, i, :size] = pieces[0]
+            mk[h, :size, :lanes] = pieces[1]
+            mv[h, :size, :lanes] = pieces[2]
+            stacked.append(jnp.concatenate(pieces, axis=1))
+        spread = jnp.dot(
+            jnp.concatenate(stacked, axis=0), bank[...], preferred_element_type=jnp.float32
+        )
+        for i in range(batch):
+            total = None
+            for b in range(4):
+                by = jnp.where(ones + turns[i][0] // 4 == b, 1.0, 0.0)
+                piece = spread[i * size : (i + 1) * size, b * lanes : (b + 1) * lanes] * by
+                total = piece if total is None else total + piece
+            fmsg[c * batch + i] = total.astype(jnp.bfloat16)
+
+    def far_send(j):
+        other = flip(me, j)
+        return remote(fmsg.at[other], frx.at[me], fs.at[j], fr.at[me], other)
+
+    def far_arrival(j):
+        other = flip(me, j)
+        return remote(fmsg.at[other], frx.at[other], fs.at[j], fr.at[other], other)
+
+    def mid_send(c):
+        return remote(mq.at[c], mqrx.at[c], ms.at[c], mr.at[c], across)
+
+    def mid_return(c):
+        return remote(mres.at[c], mret.at[c], ns.at[c], nr.at[c], across)
+
+    for j in range(devices - 1, 0, -1):
+        far_send(j).start()
+    for c in range(batches):
+        mid_send(c).start()
+    frx[me] = fmsg[me]
+
+    def attend(keys, queries, values):
+        scores = scores_of(keys, queries)
+        top = jnp.max(scores, axis=0, keepdims=True)
+        p = jnp.exp2(scores - top).astype(jnp.bfloat16)
+        return jnp.dot(values, p, preferred_element_type=jnp.float32), top
+
+    for j in range(half):
+        later_arrival(j).wait_recv()
+
+    @pl.loop(0, 4)
+    def _(t):
+        norm(1, 1, t * quarter_seats, quarter_seats)
+
+    project(1, 3, 5)
+
+    mid_lane = lax.broadcasted_iota(jnp.int32, (1, 2 * lanes), 1)
+    mid_place = (
+        jnp.where(mid_lane < lanes, me, partner) * rows
+        + (mid_lane % few) * FAR_DILATION
+        + ((mid_lane % lanes) // few) * MIDDLE_DILATION
+    )
+    mid_unit = aug_rows(jnp.ones((1, 2 * lanes), jnp.float32), 2 * lanes)
+
+    @pl.loop(0, batches)
+    def _(c):
+        for i in range(batch):
+            h = c * batch + i
+            turn, where = head_turn(h)
+            mk[h, :size, lanes:] = chosen(heads + h, rows, where)
+            mv[h, :size, lanes:] = chosen(2 * heads + h, rows, where)
+            live = mid_place + turn % MIDDLE_DILATION < valid[0]
+            mk[h, size:, :] = aug_rows(jnp.where(live, 0.0, NEGATIVE), 2 * lanes)
+            mv[h, size:, :] = aug_rows(jnp.where(live, 1.0, 0.0), 2 * lanes)
+
+    def far_return(j):
+        other = flip(me, j)
+        return remote(fres.at[other], fret.at[me], gs.at[j], gr.at[me], other)
+
+    def far_returned(j):
+        other = flip(me, j)
+        return remote(fres.at[other], fret.at[other], gs.at[j], gr.at[other], other)
+
+    def far_and_middle():
+        for j in range(1, devices):
+            far_arrival(j).wait_recv()
+
+        @pl.loop(0, devices // 4)
+        def _(g):
+            for i in range(4):
+                turned = frx[4 * g + i].T
+                at = pl.ds(pl.multiple_of((4 * g + i) * few, few), few)
+                for p, ref in enumerate((fq, fk, fv)):
+                    ref[at, :] = turned[p * few : (p + 1) * few]
+
+        my_turn = offs[me] % FAR_DILATION
+        far_size = devices * few // 2
+        far_row = lax.broadcasted_iota(jnp.int32, (devices * few, 1), 0)
+        far_live = far_row * FAR_DILATION + my_turn < valid[0]
+        sums = lax.broadcasted_iota(jnp.int32, (devices * few, AUG), 1) == 0
+
+        @pl.loop(0, 2)
+        def _(n):
+            scores = lax.dot_general(
+                fk[...], fq[pl.ds(pl.multiple_of(n * far_size, far_size), far_size), :],
+                (((1,), (1,)), ((), ())), preferred_element_type=jnp.float32,
+            )
+            scores = jnp.where(far_live, scores, NEGATIVE)
+            top = jnp.max(scores, axis=0, keepdims=True)
+            p = jnp.exp2(scores - top).astype(jnp.bfloat16)
+            count = jnp.where(far_live, jnp.where(far_row // far_size == n, 2.0, 1.0), 0.0)
+            numer = lax.dot_general(
+                (fv[...].astype(jnp.float32) * count).astype(jnp.bfloat16), p,
+                (((0,), (0,)), ((), ())), preferred_element_type=jnp.float32,
+            )
+            total = lax.dot_general(
+                jnp.where(sums, count, 0.0).astype(jnp.bfloat16), p,
+                (((0,), (0,)), ((), ())), preferred_element_type=jnp.float32,
+            )
+            sent = jnp.concatenate(
+                [numer, split_rows(total[:1], top),
+                 jnp.zeros((lanes - pad, far_size), jnp.float32)], axis=0,
+            ).T.astype(jnp.bfloat16)
+            for d in range(devices // 2):
+                fres[n * (devices // 2) + d] = sent[d * few : (d + 1) * few]
+
+        for j in range(devices - 1, 0, -1):
+            far_return(j).start()
+        fret[me] = fres[me]
+
+        @pl.loop(0, batches)
+        def _(c):
+            mid_send(c).wait_recv()
+            for i in range(batch):
+                h = c * batch + i
+                queries = jnp.concatenate(
+                    [jnp.concatenate([mq[c, i], mqrx[c, i]], axis=1), mid_unit], axis=0
+                )
+                got, top = attend(mk[h], queries, mv[h])
+                mloc[h] = got[:, :lanes]
+                mloc[h, size + 1 : size + 2, :] = top[:, :lanes]
+                mres[c, i] = jnp.concatenate(
+                    [got[:size, lanes:], split_rows(got[size : size + 1, lanes:], top[:, lanes:])],
+                    axis=0,
+                ).astype(jnp.bfloat16)
+            mid_return(c).start()
+
+    key_chunk = rows
+    key_chunks = 2 * rows // key_chunk
+
+    def scores_chunk(h, c, dst, best):
+        at = slice(c * key_chunk, (c + 1) * key_chunk)
+        scores = scores_of(qkv[heads + h, :, at], qkv[h, :, :rows])
+        dst[at, :] = scores
+        found = jnp.max(scores.reshape(key_chunk // 8, 8, rows), axis=0)
+        return found if best is None else jnp.maximum(best, found)
+
+    best = None
+    for c in range(key_chunks):
+        best = scores_chunk(0, c, s_even, best)
+    t_even[...] = jnp.max(best, axis=0, keepdims=True)
+
+    @pl.loop(0, heads // 2)
+    def _(i):
+        for u, (now, later_s, top_ref, next_top) in enumerate(
+            ((s_even, s_odd, t_even, t_odd), (s_odd, s_even, t_odd, t_even))
+        ):
+            h = 2 * i + u
+            following = 2 * i + 1 if u == 0 else (2 * i + 2) % heads
+            top = top_ref[...]
+            best = None
+            total = None
+            for c in range(key_chunks):
+                at = slice(c * key_chunk, (c + 1) * key_chunk)
+                best = scores_chunk(following, c, later_s, best)
+                p = jnp.exp2(now[at, :] - top).astype(jnp.bfloat16)
+                part = jnp.dot(qkv[2 * heads + h, :, at], p, preferred_element_type=jnp.float32)
+                total = part if total is None else total + part
+            acc[h] = total
+            acc[h, size + 1 : size + 2, :] = top
+            next_top[...] = jnp.max(best, axis=0, keepdims=True)
+
+        @pl.when(i == handle_at)
+        def _():
+            far_and_middle()
+
+    for c in range(batches):
+        mid_return(c).wait_recv()
+    for j in range(1, devices):
+        far_returned(j).wait_recv()
+
+    few_row = lax.broadcasted_iota(jnp.int32, (few, rows), 0)
+    even = column % few == few_row
+
+    def stats(a):
+        return (
+            a[size : size + 1] + a[size + 1 : size + 2],
+            a[size + 2 : size + 3] + a[size + 3 : size + 4] + a[size + 4 : size + 5],
+        )
+
+    def merge(c, i):
+        h = c * batch + i
+        turn, _ = head_turn(h)
+        in_mid = phase % MIDDLE_DILATION == turn % MIDDLE_DILATION
+        in_far = phase == turn
+        back = mret[c, i].astype(jnp.float32)
+        back_total, back_top = stats(back)
+        local_top = mloc[h, size + 1 : size + 2, :]
+        mid_top = jnp.maximum(local_top, back_top)
+        local_by = jnp.exp2(local_top - mid_top)
+        back_by = jnp.exp2(back_top - mid_top)
+        mid_total = local_by * mloc[h, size : size + 1, :] + back_by * back_total
+        mid_numer = local_by * mloc[h, :size, :] + back_by * back[:size]
+        over = lambda a: jnp.concatenate([a] * (rows // lanes), axis=1)
+        mid_top = jnp.where(in_mid, over(mid_top), NEGATIVE)
+        spread = jnp.where(in_far & even, 1.0, 0.0).astype(jnp.bfloat16)
+        far = lax.dot_general(
+            fret[h], spread, (((0,), (0,)), ((), ())), preferred_element_type=jnp.float32
+        )
+        far_total, far_top = stats(far)
+        far_top = jnp.where(in_far, far_top, NEGATIVE)
+        near_top = acc[h, size + 1 : size + 2, :]
+        top = jnp.maximum(near_top, jnp.maximum(mid_top, far_top))
+        near_by = jnp.exp2(near_top - top)
+        mid_by = jnp.where(in_mid, jnp.exp2(mid_top - top), 0.0)
+        far_by = jnp.where(in_far, jnp.exp2(far_top - top), 0.0)
+        den = near_by * acc[h, size : size + 1, :] + mid_by * over(mid_total) + far_by * far_total
+        inverse = 1.0 / jnp.maximum(den, 1.0)
+        numer = (
+            (near_by * inverse) * acc[h, :size, :]
+            + (mid_by * inverse) * over(mid_numer)
+            + (far_by * inverse) * far[:size]
+        )
+        att[pl.ds(pl.multiple_of(h * size, AUG), size), :] = numer.astype(jnp.bfloat16)
+
+    @pl.loop(0, batches)
+    def _(c):
+        for i in range(batch):
+            merge(c, i)
+
+    load_wout.wait()
+    subgain = subgain_ref[...].reshape(1, width)
+    @pl.loop(0, 2)
+    def _(c):
+        target = lax.broadcasted_iota(jnp.int32, (wide, 1), 0) + c * wide
+        order = jnp.where(place == target, 1.0, 0.0).astype(jnp.bfloat16)
+        attended = lax.dot_general(
+            order, att[...], (((1,), (1,)), ((), ())), preferred_element_type=jnp.float32
+        )
+        residual = jnp.dot(order[:, :wide], xr[0, par].reshape(wide, width), preferred_element_type=jnp.float32)
+        residual += jnp.dot(order[:, wide:], xr[1, par].reshape(wide, width), preferred_element_type=jnp.float32)
+        sub_normed = layer_norm_rows(attended, subgain).astype(jnp.bfloat16)
+        out_ref[pl.ds(pl.multiple_of(c * wide, wide), wide), :] = (
+            residual + jnp.dot(sub_normed, wout_v[...], preferred_element_type=jnp.float32)
+        ).astype(jnp.bfloat16)
+
+    for j in range(1, half):
+        first(j).wait_send()
+    for j in range(half):
+        urgent(j).wait_send()
+        later(j).wait_send()
+    for c in range(batches):
+        mid_send(c).wait_send()
+        mid_return(c).wait_send()
+    for j in range(1, devices):
+        far_send(j).wait_send()
+        far_return(j).wait_send()
+
+
+def exchanged_body(tile_embed, valid_tiles, offsets, norm_gain, w_qkv, sub_gain, w_out):
+    devices = lax.axis_size("seq")
+    rows, width = tile_embed.shape
+    heads = offsets.shape[0]
+    size = width // heads
+    pad = size + AUG
+    half = devices // 2
+    each = rows // devices
+    lanes = rows // MIDDLE_DILATION
+    few = rows // FAR_DILATION
+    scale = float(size) ** -0.5 * LOG2E
+    bf16 = lambda *shape: pltpu.VMEM(shape, jnp.bfloat16)
+    vmem = pl.BlockSpec(memory_space=pltpu.VMEM)
+    smem = pl.BlockSpec(memory_space=pltpu.SMEM)
+    anywhere = pl.BlockSpec(memory_space=pl.ANY)
+    sems = lambda n: pltpu.SemaphoreType.DMA((n,))
+    return pl.pallas_call(
+        functools.partial(layer_kernel, heads, devices, scale),
+        out_shape=jax.ShapeDtypeStruct((rows, width), jnp.bfloat16),
+        in_specs=[smem, smem, anywhere, vmem, anywhere, vmem, anywhere],
+        out_specs=vmem,
+        scratch_shapes=[
+            bf16(2, 2, half, each, width),
+            bf16(2, rows, width),
+            bf16(*w_qkv.shape),
+            bf16(*w_qkv.shape[::-1]),
+            bf16(*w_out.shape),
+            bf16(3 * heads, pad, 2 * rows),
+            pltpu.VMEM((heads, pad, rows), jnp.float32),
+            bf16(width, rows),
+            bf16(3 * lanes, 4 * lanes),
+            pltpu.VMEM((2 * rows, rows), jnp.float32),
+            pltpu.VMEM((2 * rows, rows), jnp.float32),
+            pltpu.VMEM((1, rows), jnp.float32),
+            pltpu.VMEM((1, rows), jnp.float32),
+            bf16(heads // 4, 4, size, lanes),
+            bf16(heads // 4, 4, size, lanes),
+            bf16(heads, pad, 2 * lanes),
+            bf16(heads, pad, 2 * lanes),
+            pltpu.VMEM((heads, pad, lanes), jnp.float32),
+            bf16(heads // 4, 4, pad, lanes),
+            bf16(heads // 4, 4, pad, lanes),
+            bf16(heads, size, lanes),
+            bf16(devices, size, lanes),
+            bf16(devices * few, size),
+            bf16(devices * few, size),
+            bf16(devices * few, size),
+            bf16(devices, few, lanes),
+            bf16(heads, few, lanes),
+            sems(half), sems(half), sems(half), sems(half), sems(half), sems(half),
+            sems(heads // 4), sems(heads // 4), sems(heads // 4), sems(heads // 4),
+            sems(devices), sems(devices), sems(devices), sems(devices),
+            sems(3),
+        ],
+        compiler_params=pltpu.CompilerParams(
+            vmem_limit_bytes=VMEM_LIMIT, collective_id=0, has_side_effects=True
+        ),
+        name="layer",
+    )(
+        offsets, valid_tiles, tile_embed.reshape(half, 2, each, width), norm_gain, w_qkv,
+        sub_gain, w_out,
+    )
+
+
 def solution(mesh):
+    devices = mesh.shape["seq"]
+
+    def body(tile_embed, valid_tiles, offsets, *rest):
+        fits = devices == offsets.shape[0] == FAR_DILATION and tile_embed.shape[0] % (16 * devices) == 0
+        run = exchanged_body if fits else gathered_body
+        return run(tile_embed, valid_tiles, offsets, *rest)
+
     return jax.shard_map(
         body,
         mesh=mesh,

time: 115 us -> 59.8 us (0.52)
  waiting for transfers between devices: 30.4 us -> 0 us
  starting transfers between devices: 24.4 us -> 0 us
  Pallas kernels: 44.1 us -> 56.9 us
  local copies, waits for them, and re-layouts: 14.2 us -> 2.06 us
    ppermute x11 -> x0, waiting for transfers between devices: 20 us -> none  [the longest x8 20 us: doubled(): return jnp.concatenate([rows, lax.ppermute(rows, 'seq', pairs)], axis=0)]
    ppermute x11 -> x0, starting transfers between devices: 16.1 us -> none  [the longest x8 12.8 us: doubled(): return jnp.concatenate([rows, lax.ppermute(rows, 'seq', pairs)], axis=0)]
    pallas_call x3 -> x1, Pallas kernels: 44.1 us -> 56.9 us  [exchanged_body(): pl.pallas_call(functools.partial(layer_kernel, heads, devices, scale), ou...]
    all_to_all x1 -> x0, waiting for transfers between devices: 10.4 us -> none  [body(): lax.all_to_all(pieces, 'seq', split_axis=0, concat_axis=0, tiled=True)]
    all_to_all x1 -> x0, starting transfers between devices: 8.34 us -> none  [body(): lax.all_to_all(pieces, 'seq', split_axis=0, concat_axis=0, tiled=True)]
    unnamed x22 -> x1, local copies, waits for them, and re-layouts: 7.43 us -> 2.06 us
    reshape x4 -> x0, local copies, waits for them, and re-layouts: 4.91 us -> none  [the longest x1 1.6 us: body(): sub_gain.reshape(width, 1)]
    transpose x2 -> x0, local copies, waits for them, and re-layouts: 1.8 us -> none  [the longest x1 1.74 us: body(): out.reshape(4, 4, groups, each, width).transpose(3, 2, 1, 0, 4)]
  transfers between devices with their start and end apart: 12 -> 0, of which waited for: 7 -> 0; matrix products, arithmetic and copies ran while one was open for 9% -> 0% of each run, Pallas kernels for 17% -> 0%
where the time goes in v2:
time: 59.8 us; the launch traced here: 59.7 us
  Pallas kernels  56.9 us (95%)
  local copies, waits for them, and re-layouts  2.06 us (3%)
  between operations  0.66 us (1%)
    pallas_call x1, Pallas kernels, exchanged_body(): pl.pallas_call(functools.partial(layer_kernel, heads, devices, scale), ou...  56.9 us
    unnamed x1, local copies, waits for them, and re-layouts  2.06 us

profile of v2, /device:TPU:0, one launch (start us, length us, event | category | flops | bytes accessed | tf_op | source)
XLA Modules:
  0.0 59.7 jit_solution(14199043946008503350)
XLA Ops:
  0.7 56.9 %layer.1 = bf16[512,768]{1,0:T(8,128)(2,1)} custom-call(s32[16]{0:T(128)} %offs.1, s32[1]{0:T(128)S(6)} %copy.9.valid, bf16[8,2,32,768]{3,2,1,0:T(8,128)(2,1)} %bitcast.1, f32[768]{0:T(1024)} %gain_ref.1, bf16[768,2304]{1,0:T(8,128)(2,1)} %w_hbm.1, f32[768]{0:T(1024)} %subgain_ref.1, bf16[768,768]{1,0:T(8,128)(2,1)} %wout_hbm.1), custom_call_target="tpu_custom_call" | custom-call | tf_op jit(solution)/shard_map/layer/pallas_call | solution.py:843
  57.6 2.1 %copy.10 = bf16[512,768]{1,0:T(8,128)(2,1)} copy(bf16[512,768]{1,0:T(8,128)(2,1)} %layer.1) | data formatting | bytes 1572864

commit v3 on v2

--- a/solution.py
+++ b/solution.py
@@ -393,7 +393,6 @@
     pad = size + AUG
     wide = rows // 2
     batch = 4
-    handle_at = heads // 4 - 1
     batches = heads // batch
     me = lax.axis_index("seq")
     par = me % 2
@@ -530,7 +529,7 @@
             for i in range(heads):
                 qkv[part * heads + i, :size, where] = result[i * size : (i + 1) * size]
 
-    project(0, 0, 5)
+    project(0, 0, 3)
     for j in range(half):
         urgent_arrival(j).wait_recv()
 
@@ -596,12 +595,7 @@
         mid_send(c).start()
     frx[me] = fmsg[me]
 
-    def attend(keys, queries, values):
-        scores = scores_of(keys, queries)
-        top = jnp.max(scores, axis=0, keepdims=True)
-        p = jnp.exp2(scores - top).astype(jnp.bfloat16)
-        return jnp.dot(values, p, preferred_element_type=jnp.float32), top
-
+    project(0, 3, 5)
     for j in range(half):
         later_arrival(j).wait_recv()
 
@@ -638,7 +632,7 @@
         other = flip(me, j)
         return remote(fres.at[other], fret.at[other], gs.at[j], gr.at[other], other)
 
-    def far_and_middle():
+    def far_branch():
         for j in range(1, devices):
             far_arrival(j).wait_recv()
 
@@ -685,22 +679,23 @@
             far_return(j).start()
         fret[me] = fres[me]
 
-        @pl.loop(0, batches)
-        def _(c):
-            mid_send(c).wait_recv()
-            for i in range(batch):
-                h = c * batch + i
-                queries = jnp.concatenate(
-                    [jnp.concatenate([mq[c, i], mqrx[c, i]], axis=1), mid_unit], axis=0
-                )
-                got, top = attend(mk[h], queries, mv[h])
-                mloc[h] = got[:, :lanes]
-                mloc[h, size + 1 : size + 2, :] = top[:, :lanes]
-                mres[c, i] = jnp.concatenate(
-                    [got[:size, lanes:], split_rows(got[size : size + 1, lanes:], top[:, lanes:])],
-                    axis=0,
-                ).astype(jnp.bfloat16)
-            mid_return(c).start()
+    def middle_scores(c, i):
+        queries = jnp.concatenate(
+            [jnp.concatenate([mq[c, i], mqrx[c, i]], axis=1), mid_unit], axis=0
+        )
+        return scores_of(mk[c * batch + i], queries)
+
+    def middle_rest(c, i, scores):
+        h = c * batch + i
+        top = jnp.max(scores, axis=0, keepdims=True)
+        p = jnp.exp2(scores - top).astype(jnp.bfloat16)
+        got = jnp.dot(mv[h], p, preferred_element_type=jnp.float32)
+        mloc[h] = got[:, :lanes]
+        mloc[h, size + 1 : size + 2, :] = top[:, :lanes]
+        mres[c, i] = jnp.concatenate(
+            [got[:size, lanes:], split_rows(got[size : size + 1, lanes:], top[:, lanes:])],
+            axis=0,
+        ).astype(jnp.bfloat16)
 
     key_chunk = rows
     key_chunks = 2 * rows // key_chunk
@@ -717,8 +712,7 @@
         best = scores_chunk(0, c, s_even, best)
     t_even[...] = jnp.max(best, axis=0, keepdims=True)
 
-    @pl.loop(0, heads // 2)
-    def _(i):
+    def near_pair(i):
         for u, (now, later_s, top_ref, next_top) in enumerate(
             ((s_even, s_odd, t_even, t_odd), (s_odd, s_even, t_odd, t_even))
         ):
@@ -737,9 +731,24 @@
             acc[h, size + 1 : size + 2, :] = top
             next_top[...] = jnp.max(best, axis=0, keepdims=True)
 
-        @pl.when(i == handle_at)
-        def _():
-            far_and_middle()
+    before = heads // 4
+
+    @pl.loop(0, before)
+    def _(i):
+        near_pair(i)
+
+    far_branch()
+
+    @pl.loop(0, batches)
+    def _(c):
+        mid_send(c).wait_recv()
+        for i in range(batch):
+            middle_rest(c, i, middle_scores(c, i))
+        mid_return(c).start()
+
+    @pl.loop(before, heads // 2)
+    def _(i):
+        near_pair(i)
 
     for c in range(batches):
         mid_return(c).wait_recv()

time: 59.8 us -> 59.6 us (level)
  no operation moved by 1% of the time
where the time goes in v3:
time: 59.6 us; the launch traced here: 59.4 us
  Pallas kernels  56.7 us (95%)
  local copies, waits for them, and re-layouts  2.06 us (3%)
  between operations  0.66 us (1%)
    pallas_call x1, Pallas kernels, exchanged_body(): pl.pallas_call(functools.partial(layer_kernel, heads, devices, scale), ou...  56.7 us
    unnamed x1, local copies, waits for them, and re-layouts  2.06 us

profile of v3, /device:TPU:0, one launch (start us, length us, event | category | flops | bytes accessed | tf_op | source)
XLA Modules:
  0.0 59.4 jit_solution(7881207136839036393)
XLA Ops:
  0.7 56.7 %layer.1 = bf16[512,768]{1,0:T(8,128)(2,1)} custom-call(s32[16]{0:T(128)} %offs.1, s32[1]{0:T(128)S(6)} %copy.9.valid, bf16[8,2,32,768]{3,2,1,0:T(8,128)(2,1)} %bitcast.1, f32[768]{0:T(1024)} %gain_ref.1, bf16[768,2304]{1,0:T(8,128)(2,1)} %w_hbm.1, f32[768]{0:T(1024)} %subgain_ref.1, bf16[768,768]{1,0:T(8,128)(2,1)} %wout_hbm.1), custom_call_target="tpu_custom_call" | custom-call | tf_op jit(solution)/shard_map/layer/pallas_call | solution.py:852
  57.3 2.1 %copy.10 = bf16[512,768]{1,0:T(8,128)(2,1)} copy(bf16[512,768]{1,0:T(8,128)(2,1)} %layer.1) | data formatting | bytes 1572864
